TPU v7x, 32 devices: a whole 2x2x4 slice. The times are simulated.
32 devices in a mesh: gx: 8 (over z, x), gy: 4 (over y, core).
Axes of the slice: x: 2, y: 2, z: 4, core: 2. Of those that a mesh axis runs over, the one named last changes fastest.
Arguments:
- dense_grads: float32 [32, 256, 1024], P(('gx', 'gy')), may hold values from -6 to 6
- dense_param: float32 [256, 1024], P(('gx', 'gy')), may hold values from -6 to 6
- dense_acc: float32 [256, 1024], P(('gx', 'gy'))
- table: float32 [131072, 128], P(('gx', 'gy')), may hold values from -6 to 6
- row_acc: float32 [131072], P(('gx', 'gy'))
- touched: int32 [16384], P(('gx', 'gy')), may hold values from 0 to 4095, as said below
- emb_grads: float32 [16384, 128], P(('gx', 'gy'))
Outputs:
- new_dense: float32 [256, 1024], P(('gx', 'gy'))
- new_dense_acc: float32 [256, 1024], P(('gx', 'gy'))
- new_table: float32 [131072, 128], P(('gx', 'gy'))
- new_row_acc: float32 [131072], P(('gx', 'gy'))
Inputs may be any that keep to these rules, and one draw needn't show every extreme that they name: `touched`: within one device's 512 entries no row number repeats.
All inputs are finite; a program needn't handle non-finite values.
Results may differ from a plain program's by a relative error of at most 0.000022.
Values sent between devices are 32-bit elements; how exact they have to be, the bound alone decides.
A program may use at most 128 MiB of HBM per device.

v0:
```python
import jax
import jax.numpy as jnp
from jax import lax
from jax.sharding import PartitionSpec as P

learn_rate = 0.5
max_norm = 8.0
epsilon = 1e-10


def body(dense_grads, dense_param, dense_acc, table, row_acc, touched, emb_grads):
    shards = lax.axis_size(("gx", "gy"))
    local_grad = dense_grads[0]
    embed_square = jnp.sum(emb_grads * emb_grads)
    own_rows = dense_param.shape[0]
    summed, embed_total = lax.psum((local_grad, embed_square), ("gx", "gy"))
    mean_whole = summed / jnp.float32(shards)
    norm_sq = jnp.sum(mean_whole * mean_whole) + embed_total
    start = lax.axis_index(("gx", "gy")) * own_rows
    mean_grad = lax.dynamic_slice_in_dim(mean_whole, start, own_rows, 0)
    clip = jnp.minimum(jnp.float32(1.0), max_norm / (jnp.sqrt(norm_sq) + 1e-06))
    scaled = clip * mean_grad
    new_dense_acc = dense_acc + scaled * scaled
    new_dense = dense_param - learn_rate * scaled / (jnp.sqrt(new_dense_acc) + epsilon)
    row_grads = clip * emb_grads
    square_mean = jnp.mean(row_grads * row_grads, axis=1)
    updated_acc = row_acc[touched] + square_mean
    new_row_acc = row_acc.at[touched].set(updated_acc)
    updated_rows = (
        table[touched] - learn_rate * row_grads / (jnp.sqrt(updated_acc) + epsilon)[:, None]
    )
    new_table = table.at[touched].set(updated_rows)
    return (new_dense, new_dense_acc, new_table, new_row_acc)


def solution(mesh):
    return jax.shard_map(
        body,
        mesh=mesh,
        in_specs=(
            P(("gx", "gy"), None, None),
            P(("gx", "gy"), None),
            P(("gx", "gy"), None),
            P(("gx", "gy"), None),
            P(("gx", "gy")),
            P(("gx", "gy")),
            P(("gx", "gy"), None),
        ),
        out_specs=(
            P(("gx", "gy"), None),
            P(("gx", "gy"), None),
            P(("gx", "gy"), None),
            P(("gx", "gy")),
        ),
        check_vma=False,
    )
```

profile of v0, /device:TPU:0, one launch (start us, length us, event | category | flops | bytes accessed | tf_op | source)
XLA Modules:
  0.0 165.0 jit_solution(8833698111364106730)
XLA Ops:
  7.2 0.0 all-reduce.2.cloned.1.call-start
  7.2 0.7 copy.18
  7.9 0.0 copy-start.3
  7.9 0.0 copy-start.6
  7.9 0.0 all-reduce.2.cloned.1.call-update
  8.0 0.9 copy-done.3
  8.9 0.7 multiply_reduce_fusion.2
  9.5 42.3 %psum.15 = f32[]{:T(128)} all-reduce(f32[]{:T(128)} %multiply_reduce_fusion.2), channel_id=1, replica_groups=mesh['gx'=8,'gy'=4] {'gx','gy'}, use_global_device_ids=true, to_apply=%region_3.0 | all-reduce | flops 1 | bytes 8 | tf_op jit(solution)/shard_map/psum | solution.py:16
  51.9 0.0 copy-done.6
  51.9 3.1 %gather_fusion = f32[512]{0:T(512)S(1)} fusion(f32[4096]{0:T(1024)S(1)} %copy.18, s32[1024]{0:T(1024)S(1)} %pad_clamp_fusion), kind=kCustom, calls=%fused_computation.1 | custom fusion | bytes 6144 | tf_op jit(solution)/shard_map/gather | solution.py:27
  55.0 91.9 %all-reduce.2.cloned.1.call-done = f32[256,1024]{1,0:T(8,128)} async-done(((f32[256,1024]{1,0:T(8,128)}), f32[256,1024]{1,0:T(8,128)}) %all-reduce.2.cloned.1.call-update) | async-done | bytes 1048592 | tf_op jit(solution)/shard_map/psum | solution.py:16
  147.0 2.1 %multiply_reduce_fusion = (f32[]{:T(128)}, f32[256,1024]{1,0:T(8,128)S(1)}) fusion(f32[256,1024]{1,0:T(8,128)} %all-reduce.2.cloned.1.call-done), kind=kLoop, calls=%fused_computation.4 | loop fusion | flops 786431 | bytes 2097156 | tf_op jit(solution)/shard_map/reduce_sum | solution.py:18
  150.5 0.1 multiply_reduce_fusion.1
  150.6 0.0 copy-start.2
  150.6 2.5 %scatter_fusion = f32[4096]{0:T(1024)S(1)} fusion(f32[4096]{0:T(1024)S(1)} %copy.18, s32[512]{0:T(512)S(1)} %compare_select_fusion, f32[512]{0:T(512)S(1)} %get-tuple-element.5), kind=kCustom, calls=%fused_computation.3 | custom fusion | bytes 8192 | tf_op jit(solution)/shard_map/scatter | solution.py:28
  153.1 0.0 copy-start
  153.1 0.0 copy-done.2
  153.1 0.0 copy-start.4
  153.2 0.0 copy-start.5
  153.2 3.6 %scatter_custom_fusion = f32[4096,128]{1,0:T(8,128)S(1)} fusion(f32[4096,128]{1,0:T(8,128)S(1)} %copy-done.2, s32[512]{0:T(512)S(1)} %compare_select_fusion, f32[512,128]{1,0:T(8,128)S(1)} %copy-done.3, f32[512]{0:T(512)S(1)} %get-tuple-element.4, f32[]{:T(128)} %constant.14.clone.1, f32[]{:T(128)S(6)} %min_shard_map.3, s32[1024]{0:T(1024)S(1)} %pad_clamp_fusion), kind=kCustom, calls=%fused_computation.6 | custom fusion | flops 262144 | bytes 4462600 | tf_op jit(solution)/shard_map/scatter | solution.py:32
  156.8 0.0 copy-done
  156.8 0.0 copy-start.1
  156.8 0.0 copy-done.4
  156.8 0.0 copy-done.5
  156.8 0.8 divide_subtract_fusion
  157.6 0.5 copy-done.1
  (3 shorter events, 0.0 us)
Async XLA Ops:
  7.2 139.8 %all-reduce.2.cloned.1.call-start = ((), (), s32[]{:S(2)}) async-start(), calls=%async_computation | async-start | bytes 2097152 | tf_op jit(solution)/shard_map/psum | solution.py:16
  7.9 0.9 copy-start.3
  7.9 43.9 %copy-start.6 = (s32[512]{0:T(512)S(1)}, s32[512]{0:T(512)}, u32[]{:S(2)}) copy-start(s32[512]{0:T(512)} %param.12) | copy-start | bytes 6148
  150.6 2.5 %copy-start.2 = (f32[4096,128]{1,0:T(8,128)S(1)}, f32[4096,128]{1,0:T(8,128)}, u32[]{:S(2)}) copy-start(f32[4096,128]{1,0:T(8,128)} %param.10) | copy-start | bytes 6291460
  153.1 3.7 %copy-start = (f32[4096]{0:T(1024)}, f32[4096]{0:T(1024)S(1)}, u32[]{:S(2)}) copy-start(f32[4096]{0:T(1024)S(1)} %scatter_fusion) | copy-start | bytes 49156
  153.1 3.7 %copy-start.4 = (f32[8,1024]{1,0:T(8,128)S(1)}, f32[8,1024]{1,0:T(8,128)}, u32[]{:S(2)}) copy-start(f32[8,1024]{1,0:T(8,128)} %param.8) | copy-start | bytes 98308
  153.2 3.7 %copy-start.5 = (f32[8,1024]{1,0:T(8,128)S(1)}, f32[8,1024]{1,0:T(8,128)}, u32[]{:S(2)}) copy-start(f32[8,1024]{1,0:T(8,128)} %param.9) | copy-start | bytes 98308
  156.8 1.3 copy-start.1
Sparse Core Ops, SparseCore 0:
  13.2 133.7 all-reduce.1
where the time goes:
time: 165 us
  waiting for transfers between devices  92 us (56%)
  blocking collectives  42.3 us (26%)
  between operations  15.5 us (9%)
  local copies, waits for them, and re-layouts  7.84 us (5%)
  other arithmetic  7.32 us (4%)
    psum x1, waiting for transfers between devices, body(): summed, embed_total = lax.psum((local_grad, embed_square), ('gx', 'gy'))  91.9 us
    psum x1, blocking collectives, body(): summed, embed_total = lax.psum((local_grad, embed_square), ('gx', 'gy'))  42.3 us
    scatter x1, other arithmetic, body(): new_table = table.at[touched].set(updated_rows)  3.6 us
  transfers between devices with their start and end apart: 1, of which 1 were waited for; matrix products, arithmetic and copies ran while one was open for 2% of the time, Pallas kernels for 0%

commit v1 on v0

--- a/solution.py
+++ b/solution.py
@@ -13,7 +13,7 @@
     local_grad = dense_grads[0]
     embed_square = jnp.sum(emb_grads * emb_grads)
     own_rows = dense_param.shape[0]
-    summed, embed_total = lax.psum((local_grad, embed_square), ("gx", "gy"))
+    summed, embed_total = lax.psum(lax.psum((local_grad, embed_square), "gy"), "gx")
     mean_whole = summed / jnp.float32(shards)
     norm_sq = jnp.sum(mean_whole * mean_whole) + embed_total
     start = lax.axis_index(("gx", "gy")) * own_rows

time: 165 us -> 150 us (0.909)
  blocking collectives: 42.3 us -> 28.8 us
    psum x1 -> x2, blocking collectives: 42.3 us -> 28.8 us  [the longest x1 22.3 us: body(): lax.psum(lax.psum((local_grad, embed_square), 'gy'), 'gx')]
    psum x1 -> x2, waiting for transfers between devices: 91.9 us -> 91 us  [the longest x1 49.6 us: body(): lax.psum(lax.psum((local_grad, embed_square), 'gy'), 'gx')]
  transfers between devices with their start and end apart: 1 -> 2, of which waited for: 1 -> 2; matrix products, arithmetic and copies ran while one was open for 2% -> 3% of each run, Pallas kernels for 0% -> 0%
where the time goes in v1:
time: 150 us
  waiting for transfers between devices  91 us (61%)
  blocking collectives  28.8 us (19%)
  between operations  15.5 us (10%)
  other arithmetic  7.31 us (5%)
  local copies, waits for them, and re-layouts  6.93 us (5%)
    psum x1, waiting for transfers between devices, body(): lax.psum(lax.psum((local_grad, embed_square), 'gy'), 'gx')  49.6 us
    psum x1, waiting for transfers between devices, body(): lax.psum((local_grad, embed_square), 'gy')  41.4 us
    psum x1, blocking collectives, body(): lax.psum(lax.psum((local_grad, embed_square), 'gy'), 'gx')  22.3 us
    psum x1, blocking collectives, body(): lax.psum((local_grad, embed_square), 'gy')  6.52 us
    scatter x1, other arithmetic, body(): new_table = table.at[touched].set(updated_rows)  3.6 us
    gather x1, local copies, waits for them, and re-layouts, body(): updated_acc = row_acc[touched] + square_mean  3.14 us
  transfers between devices with their start and end apart: 2, of which 2 were waited for; matrix products, arithmetic and copies ran while one was open for 3% of the time, Pallas kernels for 0%

profile of v1, /device:TPU:0, one launch (start us, length us, event | category | flops | bytes accessed | tf_op | source)
XLA Modules:
  0.0 149.7 jit_solution(11305364697682878015)
XLA Ops:
  7.2 0.0 all-reduce.3.cloned.1.call-start
  7.2 0.7 copy.19
  7.9 0.0 copy-start.3
  7.9 0.0 copy-start.6
  7.9 0.0 all-reduce.3.cloned.1.call-update
  8.0 0.0 all-reduce.5.cloned.1.call-start
  8.0 41.4 %all-reduce.3.cloned.1.call-done = f32[256,1024]{1,0:T(8,128)} async-done(((f32[256,1024]{1,0:T(8,128)}), f32[256,1024]{1,0:T(8,128)}) %all-reduce.3.cloned.1.call-update) | async-done | bytes 1048592 | tf_op jit(solution)/shard_map/psum | solution.py:16
  49.4 0.0 all-reduce.5.cloned.1.call-update
  49.4 0.0 copy-done.3
  49.4 0.7 multiply_reduce_fusion.2
  50.1 6.5 %psum.30 = f32[]{:T(128)} all-reduce(f32[]{:T(128)} %multiply_reduce_fusion.2), channel_id=1, replica_groups=mesh['gx'=8,'gy'=4] {'gy'}, use_global_device_ids=true, to_apply=%region_4.0 | all-reduce | flops 1 | bytes 8 | tf_op jit(solution)/shard_map/psum | solution.py:16
  56.6 22.3 %psum.31 = f32[]{:T(128)} all-reduce(f32[]{:T(128)} %psum.30), channel_id=1, replica_groups=mesh['gx'=8,'gy'=4] {'gx'}, use_global_device_ids=true, to_apply=%region_5.0 | all-reduce | flops 1 | bytes 8 | tf_op jit(solution)/shard_map/psum | solution.py:16
  78.9 0.0 copy-done.6
  78.9 3.1 %gather_fusion = f32[512]{0:T(512)S(1)} fusion(f32[4096]{0:T(1024)S(1)} %copy.19, s32[1024]{0:T(1024)S(1)} %pad_clamp_fusion), kind=kCustom, calls=%fused_computation.1 | custom fusion | bytes 6144 | tf_op jit(solution)/shard_map/gather | solution.py:27
  82.1 49.6 %all-reduce.5.cloned.1.call-done = f32[256,1024]{1,0:T(8,128)} async-done(((f32[256,1024]{1,0:T(8,128)}), f32[256,1024]{1,0:T(8,128)}) %all-reduce.5.cloned.1.call-update) | async-done | bytes 1048592 | tf_op jit(solution)/shard_map/psum | solution.py:16
  131.7 2.1 %multiply_reduce_fusion = (f32[]{:T(128)}, f32[256,1024]{1,0:T(8,128)S(1)}) fusion(f32[256,1024]{1,0:T(8,128)} %all-reduce.5.cloned.1.call-done), kind=kLoop, calls=%fused_computation.4 | loop fusion | flops 786431 | bytes 2097156 | tf_op jit(solution)/shard_map/reduce_sum | solution.py:18
  135.2 0.1 multiply_reduce_fusion.1
  135.4 0.0 copy-start.2
  135.4 2.5 %scatter_fusion = f32[4096]{0:T(1024)S(1)} fusion(f32[4096]{0:T(1024)S(1)} %copy.19, s32[512]{0:T(512)S(1)} %compare_select_fusion, f32[512]{0:T(512)S(1)} %get-tuple-element.5), kind=kCustom, calls=%fused_computation.3 | custom fusion | bytes 8192 | tf_op jit(solution)/shard_map/scatter | solution.py:28
  137.9 0.0 copy-start
  137.9 0.0 copy-done.2
  137.9 0.0 copy-start.4
  137.9 0.0 copy-start.5
  137.9 3.6 %scatter_custom_fusion = f32[4096,128]{1,0:T(8,128)S(1)} fusion(f32[4096,128]{1,0:T(8,128)S(1)} %copy-done.2, s32[512]{0:T(512)S(1)} %compare_select_fusion, f32[512,128]{1,0:T(8,128)S(1)} %copy-done.3, f32[512]{0:T(512)S(1)} %get-tuple-element.4, f32[]{:T(128)} %constant.14.clone.1, f32[]{:T(128)S(6)} %min_shard_map.3, s32[1024]{0:T(1024)S(1)} %pad_clamp_fusion), kind=kCustom, calls=%fused_computation.6 | custom fusion | flops 262144 | bytes 4462600 | tf_op jit(solution)/shard_map/scatter | solution.py:32
  141.5 0.0 copy-done
  141.5 0.0 copy-start.1
  141.5 0.0 copy-done.4
  141.6 0.0 copy-done.5
  141.6 0.8 divide_subtract_fusion
  142.3 0.5 copy-done.1
  (3 shorter events, 0.0 us)
Async XLA Ops:
  7.2 42.2 %all-reduce.3.cloned.1.call-start = ((), (), s32[]{:S(2)}) async-start(), calls=%async_computation | async-start | bytes 2097152 | tf_op jit(solution)/shard_map/psum | solution.py:16
  7.9 41.5 %copy-start.3 = (f32[512,128]{1,0:T(8,128)S(1)}, f32[512,128]{1,0:T(8,128)}, u32[]{:S(2)}) copy-start(f32[512,128]{1,0:T(8,128)} %param.13) | copy-start | bytes 786436
  7.9 71.0 %copy-start.6 = (s32[512]{0:T(512)S(1)}, s32[512]{0:T(512)}, u32[]{:S(2)}) copy-start(s32[512]{0:T(512)} %param.12) | copy-start | bytes 6148
  8.0 123.7 %all-reduce.5.cloned.1.call-start = ((), (), s32[]{:S(2)}) async-start(), calls=%async_computation.1 | async-start | bytes 2097152 | tf_op jit(solution)/shard_map/psum | solution.py:16
  135.4 2.5 %copy-start.2 = (f32[4096,128]{1,0:T(8,128)S(1)}, f32[4096,128]{1,0:T(8,128)}, u32[]{:S(2)}) copy-start(f32[4096,128]{1,0:T(8,128)} %param.10) | copy-start | bytes 6291460
  137.9 3.7 %copy-start = (f32[4096]{0:T(1024)}, f32[4096]{0:T(1024)S(1)}, u32[]{:S(2)}) copy-start(f32[4096]{0:T(1024)S(1)} %scatter_fusion) | copy-start | bytes 49156
  137.9 3.7 %copy-start.4 = (f32[8,1024]{1,0:T(8,128)S(1)}, f32[8,1024]{1,0:T(8,128)}, u32[]{:S(2)}) copy-start(f32[8,1024]{1,0:T(8,128)} %param.8) | copy-start | bytes 98308
  137.9 3.7 %copy-start.5 = (f32[8,1024]{1,0:T(8,128)S(1)}, f32[8,1024]{1,0:T(8,128)}, u32[]{:S(2)}) copy-start(f32[8,1024]{1,0:T(8,128)} %param.9) | copy-start | bytes 98308
  141.5 1.3 copy-start.1
Sparse Core Ops, SparseCore 0:
  10.3 38.9 all-reduce.2
  52.9 78.7 all-reduce.4
